TPU v7x, 32 devices: a whole 2x2x4 slice. The times are simulated.
32 devices in a mesh: row: 4 (over y, x), col: 2 (over core), layer: 4 (over z).
Axes of the slice: x: 2, y: 2, z: 4, core: 2. Of those that a mesh axis runs over, the one named last changes fastest.
Arguments:
- matrix: float32 [4096, 4096], P('row', 'col'), may hold values from -6 to 6
- pattern: int32 [128, 128], P('row', 'col'), may hold values 0 or 1
- keep: int32 [128, 128], P('row', 'col'), may hold values 0 or 1
Outputs:
- update: float32 [4096, 4096], P(('row', 'layer'), 'col')
All inputs are finite; a program needn't handle non-finite values. No bound on the sum of `pattern` or of `keep` on one device may be relied on, other than what follows from the above.
Results may differ from a plain program's by a relative error of at most 0.00005.
Values sent between devices are 32-bit elements; how exact they have to be, the bound alone decides.
A program may use at most 128 MiB of HBM per device.

v0:
```python
import jax
import jax.numpy as jnp
from jax import lax
from jax.sharding import PartitionSpec as P

BS = 32
NB = 128


def layer_rows(values, layers, level):
    count, width = values.shape
    shaped = values.reshape(count // (layers * BS), layers, BS, width)
    picked = lax.dynamic_index_in_dim(shaped, level, 1, keepdims=False)
    return picked.reshape(count // layers, width)


def local(matrix, pattern, keep):
    rows, cols = matrix.shape
    block_rows, block_cols = pattern.shape
    layers = lax.axis_size("layer")
    level = lax.axis_index("layer")
    sparse = (
        matrix.reshape(block_rows, BS, block_cols, BS)
        * pattern.astype(jnp.float32)[:, None, :, None]
    ).reshape(rows, cols)
    left_local = lax.dynamic_index_in_dim(
        sparse.reshape(rows, block_cols // layers, layers, BS), level, 2, keepdims=False
    )
    left_local = left_local.reshape(rows, block_cols // layers * BS)
    left_full = lax.all_gather(left_local, "col", axis=1, tiled=True)
    right_full = lax.all_gather(layer_rows(sparse, layers, level), "row", axis=0, tiled=True)
    partial_value = jnp.dot(
        left_full, right_full, preferred_element_type=jnp.float32, precision=lax.Precision.HIGHEST
    )
    keep_flags = keep.astype(jnp.float32)
    keep_mine = lax.dynamic_index_in_dim(
        keep_flags.reshape(block_rows // layers, layers, block_cols), level, 1, keepdims=False
    )
    square = lax.psum(partial_value, "layer")
    mine = layer_rows(square, layers, level)
    filtered = (
        mine.reshape(block_rows // layers, BS, block_cols, BS) * keep_mine[:, None, :, None]
    ).reshape(rows // layers, cols)
    filtered_full = lax.all_gather(filtered, "row", axis=0, tiled=True)
    share = rows // layers
    summed = lax.psum_scatter(
        jnp.dot(
            left_full,
            filtered_full,
            preferred_element_type=jnp.float32,
            precision=lax.Precision.HIGHEST,
        ),
        "layer",
        scatter_dimension=0,
        tiled=True,
    )
    own_rows = lax.dynamic_slice_in_dim(sparse, level * share, share, 0)
    factor = 0.72 / (NB * BS)
    return 1.5 * own_rows - 0.5 * factor * summed


def solution(mesh):
    placed = (P("row", "col"), P("row", "col"), P("row", "col"))
    return jax.shard_map(
        local, mesh=mesh, in_specs=placed, out_specs=P(("row", "layer"), "col"), check_vma=False
    )
```

profile of v0, /device:TPU:0, one launch (start us, length us, event | category | flops | bytes accessed | tf_op | source)
XLA Modules:
  0.0 727.2 jit_solution(3081529053856967968)
XLA Ops:
  6.5 0.0 all-gather.4.cloned.1.call-start
  6.5 0.7 convert_element_type.6
  7.3 9.3 %copy.4 = f32[1024,2048]{0,1:T(8,128)} copy(f32[1024,2048]{1,0:T(8,128)} %param.3) | data formatting | bytes 16777216 | tf_op args[0]
  16.5 0.1 copy.5
  16.6 0.3 mul.63
  16.9 0.5 mul.64
  17.4 0.1 constant_dynamic-slice_fusion.3
  17.5 3.3 dynamic-slice_multiply_fusion.1
  20.8 0.0 all-gather.4.cloned.1.call-update
  20.8 0.0 all-gather.6.cloned.1.call-start
  20.9 0.3 mul.67
  21.2 0.5 mul.68
  21.7 0.1 constant_dynamic-slice_fusion.2
  21.8 3.2 dynamic-slice_multiply_fusion
  25.0 0.0 all-gather.6.cloned.1.call-update
  25.0 0.0 all-reduce.2.cloned.1.call-start
  25.1 12.3 %all-gather.4.cloned.1.call-done = f32[1024,1024]{0,1:T(8,128)} async-done(((f32[1024,512]{0,1:T(8,128)}), f32[1024,1024]{0,1:T(8,128)}) %all-gather.4.cloned.1.call-update) | async-done | bytes 4194320 | tf_op jit(solution)/shard_map/all_gather | solution.py:30
  37.4 90.5 %all-gather.6.cloned.1.call-done = f32[1024,2048]{1,0:T(8,128)} async-done(((f32[256,2048]{1,0:T(8,128)}), f32[1024,2048]{1,0:T(8,128)}) %all-gather.6.cloned.1.call-update) | async-done | bytes 8388624 | tf_op jit(solution)/shard_map/all_gather | solution.py:31
  127.9 31.0 %fusion.2 = f32[1024,2048]{1,0:T(8,128)} fusion(f32[1024,1024]{0,1:T(8,128)} %all-gather.4.cloned.1.call-done, f32[1024,2048]{1,0:T(8,128)} %all-gather.6.cloned.1.call-done), kind=kOutput, calls=%fused_computation.10 | convolution fusion | flops 25769803776 | bytes 20971520 | tf_op jit(solution)/shard_map/dot_general | solution.py:32
  158.9 0.0 copy-start
  158.9 0.0 all-reduce.2.cloned.1.call-update
  159.0 0.0 all-gather.8.cloned.1.call-start
  159.0 0.6 copy-done
  159.7 4.4 mul.72
  164.0 6.9 mul.73
  170.9 279.0 %all-reduce.2.cloned.1.call-done = f32[8,4,32,2048]{3,2,1,0:T(8,128)} async-done(((f32[8,4,32,2048]{3,2,1,0:T(8,128)}), f32[8,4,32,2048]{3,2,1,0:T(8,128)}) %all-reduce.2.cloned.1.call-update) | async-done | bytes 8388624 | tf_op jit(solution)/shard_map/psum | solution.py:39
  449.9 1.7 constant_dynamic-slice_fusion.1
  451.7 1.6 bitcast_multiply_fusion
  453.3 0.0 all-gather.8.cloned.1.call-update
  453.3 0.2 reduce-scatter.2.cloned.1.call-start
  453.5 86.4 %all-gather.8.cloned.1.call-done = f32[1024,2048]{1,0:T(8,128)} async-done(((f32[256,2048]{1,0:T(8,128)}), f32[1024,2048]{1,0:T(8,128)}) %all-gather.8.cloned.1.call-update) | async-done | bytes 8388624 | tf_op jit(solution)/shard_map/all_gather | solution.py:44
  539.9 31.0 %fusion.3 = f32[1024,2048]{1,0:T(8,128)} fusion(f32[1024,1024]{0,1:T(8,128)} %all-gather.4.cloned.1.call-done, f32[1024,2048]{1,0:T(8,128)} %all-gather.8.cloned.1.call-done), kind=kOutput, calls=%fused_computation.11 | convolution fusion | flops 25769803776 | bytes 20971520 | tf_op jit(solution)/shard_map/dot_general | solution.py:47
  571.0 0.0 reduce-scatter.2.cloned.1.call-update
  571.0 11.7 %mul.57 = f32[32,32,64,32]{3,2,1,0:T(8,128)} broadcast(f32[32,64]{1,0:T(8,128)S(1)} %convert_element_type.6), dimensions={0,2} | broadcast | bytes 8396800 | tf_op jit(solution)/shard_map/mul | solution.py:23
  582.6 25.5 %mul.58 = f32[1024,2048]{1,0:T(8,128)} reshape(f32[32,32,64,32]{3,2,1,0:T(8,128)} %mul.57) | data formatting | bytes 16777216 | tf_op jit(solution)/shard_map/mul | solution.py:23
  608.1 107.7 %reduce-scatter.2.cloned.1.call-done = f32[256,2048]{1,0:T(8,128)} async-done(((f32[1024,2048]{1,0:T(8,128)}), f32[256,2048]{1,0:T(8,128)}) %reduce-scatter.2.cloned.1.call-update) | async-done | bytes 2097168 | tf_op jit(solution)/shard_map/reduce_scatter | solution.py:46
  715.7 5.0 fusion.1
  (2 shorter events, 0.0 us)
Async XLA Ops:
  6.5 30.8 %all-gather.4.cloned.1.call-start = ((), (), s32[]{:S(2)}) async-start(), calls=%async_computation.1 | async-start | bytes 6291456 | tf_op jit(solution)/shard_map/all_gather | solution.py:30
  20.8 107.1 %all-gather.6.cloned.1.call-start = ((), (), s32[]{:S(2)}) async-start(), calls=%async_computation.2 | async-start | bytes 10485760 | tf_op jit(solution)/shard_map/all_gather | solution.py:31
  25.0 424.9 %all-reduce.2.cloned.1.call-start = ((), (), s32[]{:S(2)}) async-start(), calls=%async_computation.3 | async-start | bytes 16777216 | tf_op jit(solution)/shard_map/psum | solution.py:39
  158.9 0.7 copy-start
  159.0 381.0 %all-gather.8.cloned.1.call-start = ((), (), s32[]{:S(2)}) async-start(), calls=%async_computation.4 | async-start | bytes 10485760 | tf_op jit(solution)/shard_map/all_gather | solution.py:44
  453.3 262.4 %reduce-scatter.2.cloned.1.call-start = ((), (), s32[]{:S(2)}) async-start(), calls=%async_computation.5 | async-start | bytes 10485760 | tf_op jit(solution)/shard_map/reduce_scatter | solution.py:46
Sparse Core Ops, SparseCore 0:
  20.9 16.3 all-gather.3
  39.2 88.6 all-gather.5
  159.1 290.8 all-reduce.1
  453.4 86.4 all-gather.7
  571.1 144.6 reduce-scatter.1
where the time goes:
time: 728 us; the launch traced here: 727 us
  waiting for transfers between devices  576 us (79%)
  matrix products  62.1 us (9%)
  local copies, waits for them, and re-layouts  61.9 us (9%)
  other arithmetic  13.8 us (2%)
  between operations  13.2 us (2%)
    psum x1, waiting for transfers between devices, local(): square = lax.psum(partial_value, 'layer')  279 us
    reduce_scatter x1, waiting for transfers between devices, local(): lax.psum_scatter(jnp.dot(left_full, filtered_full, preferred_element_type...  108 us
    all_gather x1, waiting for transfers between devices, local(): lax.all_gather(layer_rows(sparse, layers, level), 'row', axis=0, tiled=True)  90.5 us
    all_gather x1, waiting for transfers between devices, local(): filtered_full = lax.all_gather(filtered, 'row', axis=0, tiled=True)  86.4 us
    mul x6, local copies, waits for them, and re-layouts, local(): matrix.reshape(block_rows, BS, block_cols, BS)  38.8 us
    dot_general x1, matrix products, local(): jnp.dot(left_full, right_full, preferred_element_type=jnp.float32, precis...  31 us
    dot_general x1, matrix products, local(): jnp.dot(left_full, filtered_full, preferred_element_type=jnp.float32, pre...  31 us
  transfers between devices with their start and end apart: 5, of which 5 were waited for; matrix products, arithmetic and copies ran while one was open for 7% of the time, Pallas kernels for 0%

commit v1 on v0

--- a/solution.py
+++ b/solution.py
@@ -5,6 +5,11 @@
 
 BS = 32
 NB = 128
+
+
+def gather_and_add(x, mesh_axis):
+    parts = lax.all_gather(x, mesh_axis)
+    return jnp.sum(parts, axis=0)
 
 
 def layer_rows(values, layers, level):
@@ -36,7 +41,7 @@
     keep_mine = lax.dynamic_index_in_dim(
         keep_flags.reshape(block_rows // layers, layers, block_cols), level, 1, keepdims=False
     )
-    square = lax.psum(partial_value, "layer")
+    square = gather_and_add(partial_value, "layer")
     mine = layer_rows(square, layers, level)
     filtered = (
         mine.reshape(block_rows // layers, BS, block_cols, BS) * keep_mine[:, None, :, None]

time: 728 us -> 1010 us (1.39)
  waiting for transfers between devices: 576 us -> 845 us
  other arithmetic: 13.8 us -> 29.8 us
    all_gather x0 -> x1, waiting for transfers between devices: none -> 549 us  [gather_and_add(): parts = lax.all_gather(x, mesh_axis)]
    psum x1 -> x0, waiting for transfers between devices: 279 us -> none  [local(): square = lax.psum(partial_value, 'layer')]
    reduce_sum x0 -> x1, other arithmetic: none -> 15.9 us  [gather_and_add(): return jnp.sum(parts, axis=0)]
  transfers between devices with their start and end apart: 5 -> 5, of which waited for: 5 -> 5; matrix products, arithmetic and copies ran while one was open for 7% -> 5% of each run, Pallas kernels for 0% -> 0%
where the time goes in v1:
time: 1010 us
  waiting for transfers between devices  845 us (84%)
  local copies, waits for them, and re-layouts  62.3 us (6%)
  matrix products  62.1 us (6%)
  other arithmetic  29.8 us (3%)
  between operations  13.2 us (1%)
    all_gather x1, waiting for transfers between devices, gather_and_add(): parts = lax.all_gather(x, mesh_axis)  549 us
    reduce_scatter x1, waiting for transfers between devices, local(): lax.psum_scatter(jnp.dot(left_full, filtered_full, preferred_element_type...  108 us
    all_gather x1, waiting for transfers between devices, local(): lax.all_gather(layer_rows(sparse, layers, level), 'row', axis=0, tiled=True)  90.5 us
    all_gather x1, waiting for transfers between devices, local(): filtered_full = lax.all_gather(filtered, 'row', axis=0, tiled=True)  85.8 us
    mul x6, local copies, waits for them, and re-layouts, local(): matrix.reshape(block_rows, BS, block_cols, BS)  38.8 us
    dot_general x1, matrix products, local(): jnp.dot(left_full, filtered_full, preferred_element_type=jnp.float32, pre...  31 us
    dot_general x1, matrix products, local(): jnp.dot(left_full, right_full, preferred_element_type=jnp.float32, precis...  31 us
  transfers between devices with their start and end apart: 5, of which 5 were waited for; matrix products, arithmetic and copies ran while one was open for 5% of the time, Pallas kernels for 0%

profile of v1, /device:TPU:0, one launch (start us, length us, event | category | flops | bytes accessed | tf_op | source)
XLA Modules:
  0.0 1012.9 jit_solution(5552732197705775513)
XLA Ops:
  6.5 0.0 all-gather.6.cloned.1.call-start
  6.5 0.7 convert_element_type.6
  7.3 0.1 copy.7
  7.3 0.3 mul.63
  7.7 0.5 mul.64
  8.2 9.3 copy.6
  17.5 0.1 constant_dynamic-slice_fusion.3
  17.5 3.3 dynamic-slice_multiply_fusion.1
  20.8 0.0 all-gather.6.cloned.1.call-update
  20.8 0.0 all-gather.8.cloned.1.call-start
  20.9 0.3 mul.67
  21.2 0.5 mul.68
  21.7 0.1 constant_dynamic-slice_fusion.2
  21.8 3.3 dynamic-slice_multiply_fusion
  25.0 0.0 all-gather.8.cloned.1.call-update
  25.1 0.0 all-gather.12.cloned.1.call-start
  25.1 12.3 %all-gather.6.cloned.1.call-done = f32[1024,1024]{0,1:T(8,128)} async-done(((f32[1024,512]{0,1:T(8,128)}), f32[1024,1024]{0,1:T(8,128)}) %all-gather.6.cloned.1.call-update) | async-done | bytes 4194320 | tf_op jit(solution)/shard_map/all_gather | solution.py:35
  37.4 90.5 %all-gather.8.cloned.1.call-done = f32[1024,2048]{1,0:T(8,128)} async-done(((f32[256,2048]{1,0:T(8,128)}), f32[1024,2048]{1,0:T(8,128)}) %all-gather.8.cloned.1.call-update) | async-done | bytes 8388624 | tf_op jit(solution)/shard_map/all_gather | solution.py:36
  127.9 31.0 %fusion.2 = f32[1024,2048]{1,0:T(8,128)} fusion(f32[1024,1024]{0,1:T(8,128)} %all-gather.6.cloned.1.call-done, f32[1024,2048]{1,0:T(8,128)} %all-gather.8.cloned.1.call-done), kind=kOutput, calls=%fused_computation.10 | convolution fusion | flops 25769803776 | bytes 20971520 | tf_op jit(solution)/shard_map/dot_general | solution.py:37
  158.9 0.0 copy-start
  158.9 0.0 all-gather.12.cloned.1.call-update
  159.0 0.2 all-gather.10.cloned.1.call-start
  159.2 0.5 copy-done
  159.7 4.3 mul.72
  164.0 7.4 mul.73
  171.5 549.0 %all-gather.12.cloned.1.call-done = f32[4096,2048]{1,0:T(8,128)} async-done(((f32[1024,2048]{1,0:T(8,128)}), f32[4096,2048]{1,0:T(8,128)}) %all-gather.12.cloned.1.call-update) | async-done | bytes 33554448 | tf_op jit(solution)/shard_map/all_gather | solution.py:11
  720.5 15.9 %reduce_sum.9 = f32[1024,2048]{1,0:T(8,128)} reduce(f32[4,1024,2048]{2,1,0:T(8,128)} %bitcast.20, f32[]{:T(128)} %constant.29.clone.1), dimensions={0}, to_apply=%region_0.1 | reduce | flops 6291456 | bytes 41943044 | tf_op jit(solution)/shard_map/reduce_sum | solution.py:12
  736.4 1.7 constant_dynamic-slice_fusion.1
  738.2 1.6 bitcast_multiply_fusion
  739.8 0.0 all-gather.10.cloned.1.call-update
  739.8 0.0 reduce-scatter.2.cloned.1.call-start
  739.8 85.8 %all-gather.10.cloned.1.call-done = f32[1024,2048]{1,0:T(8,128)} async-done(((f32[256,2048]{1,0:T(8,128)}), f32[1024,2048]{1,0:T(8,128)}) %all-gather.10.cloned.1.call-update) | async-done | bytes 8388624 | tf_op jit(solution)/shard_map/all_gather | solution.py:49
  825.6 31.0 %fusion.3 = f32[1024,2048]{1,0:T(8,128)} fusion(f32[1024,1024]{0,1:T(8,128)} %all-gather.6.cloned.1.call-done, f32[1024,2048]{1,0:T(8,128)} %all-gather.10.cloned.1.call-done), kind=kOutput, calls=%fused_computation.11 | convolution fusion | flops 25769803776 | bytes 20971520 | tf_op jit(solution)/shard_map/dot_general | solution.py:52
  856.6 0.0 reduce-scatter.2.cloned.1.call-update
  856.7 11.7 %mul.57 = f32[32,32,64,32]{3,2,1,0:T(8,128)} broadcast(f32[32,64]{1,0:T(8,128)S(1)} %convert_element_type.6), dimensions={0,2} | broadcast | bytes 8396800 | tf_op jit(solution)/shard_map/mul | solution.py:28
  868.3 25.5 %mul.58 = f32[1024,2048]{1,0:T(8,128)} reshape(f32[32,32,64,32]{3,2,1,0:T(8,128)} %mul.57) | data formatting | bytes 16777216 | tf_op jit(solution)/shard_map/mul | solution.py:28
  893.8 107.7 %reduce-scatter.2.cloned.1.call-done = f32[256,2048]{1,0:T(8,128)} async-done(((f32[1024,2048]{1,0:T(8,128)}), f32[256,2048]{1,0:T(8,128)}) %reduce-scatter.2.cloned.1.call-update) | async-done | bytes 2097168 | tf_op jit(solution)/shard_map/reduce_scatter | solution.py:51
  1001.4 5.0 fusion.1
  (2 shorter events, 0.0 us)
Async XLA Ops:
  6.5 30.8 %all-gather.6.cloned.1.call-start = ((), (), s32[]{:S(2)}) async-start(), calls=%async_computation.1 | async-start | bytes 6291456 | tf_op jit(solution)/shard_map/all_gather | solution.py:35
  20.8 107.1 %all-gather.8.cloned.1.call-start = ((), (), s32[]{:S(2)}) async-start(), calls=%async_computation.2 | async-start | bytes 10485760 | tf_op jit(solution)/shard_map/all_gather | solution.py:36
  25.1 695.4 %all-gather.12.cloned.1.call-start = ((), (), s32[]{:S(2)}) async-start(), calls=%async_computation.5 | async-start | bytes 41943040 | tf_op jit(solution)/shard_map/all_gather | solution.py:11
  158.9 0.7 copy-start
  159.0 666.7 %all-gather.10.cloned.1.call-start = ((), (), s32[]{:S(2)}) async-start(), calls=%async_computation.3 | async-start | bytes 10485760 | tf_op jit(solution)/shard_map/all_gather | solution.py:49
  739.8 261.6 %reduce-scatter.2.cloned.1.call-start = ((), (), s32[]{:S(2)}) async-start(), calls=%async_computation.4 | async-start | bytes 10485760 | tf_op jit(solution)/shard_map/reduce_scatter | solution.py:51
Sparse Core Ops, SparseCore 0:
  20.9 16.3 all-gather.5
  39.2 88.6 all-gather.7
  159.1 561.3 all-gather.11
  739.9 85.6 all-gather.9
  856.8 144.6 reduce-scatter.1

commit v2 on v0

--- a/solution.py
+++ b/solution.py
@@ -5,6 +5,16 @@
 
 BS = 32
 NB = 128
+
+
+def turned_line(block, axis, dim):
+    size = lax.axis_size(axis)
+    current, blocks = (block, [block])
+    for _ in range(size - 1):
+        current = lax.ppermute(current, axis, [(i, (i + 1) % size) for i in range(size)])
+        blocks.insert(0, current)
+    line = jnp.concatenate(blocks, axis=dim)
+    return jnp.roll(line, (lax.axis_index(axis) + 1) * block.shape[dim], axis=dim)
 
 
 def layer_rows(values, layers, level):
@@ -41,7 +51,7 @@
     filtered = (
         mine.reshape(block_rows // layers, BS, block_cols, BS) * keep_mine[:, None, :, None]
     ).reshape(rows // layers, cols)
-    filtered_full = lax.all_gather(filtered, "row", axis=0, tiled=True)
+    filtered_full = turned_line(filtered, "row", 0)
     share = rows // layers
     summed = lax.psum_scatter(
         jnp.dot(

time: 728 us -> 790 us (1.085)
  waiting for transfers between devices: 576 us -> 628 us
  local copies, waits for them, and re-layouts: 61.9 us -> 72.2 us
    ppermute x0 -> x3, waiting for transfers between devices: none -> 140 us  [turned_line(): lax.ppermute(current, axis, [(i, (i + 1) % size) for i in range(size)])]
    all_gather x1 -> x0, waiting for transfers between devices: 86.4 us -> none  [local(): filtered_full = lax.all_gather(filtered, 'row', axis=0, tiled=True)]
    unnamed x3 -> x16, local copies, waits for them, and re-layouts: 9.92 us -> 19.1 us
  transfers between devices with their start and end apart: 5 -> 7, of which waited for: 5 -> 7; matrix products, arithmetic and copies ran while one was open for 7% -> 7% of each run, Pallas kernels for 0% -> 0%
where the time goes in v2:
time: 790 us; the launch traced here: 789 us
  waiting for transfers between devices  628 us (79%)
  local copies, waits for them, and re-layouts  72.2 us (9%)
  matrix products  60.1 us (8%)
  other arithmetic  14 us (2%)
  between operations  13.3 us (2%)
    psum x1, waiting for transfers between devices, local(): square = lax.psum(partial_value, 'layer')  278 us
    ppermute x3, waiting for transfers between devices, turned_line(): lax.ppermute(current, axis, [(i, (i + 1) % size) for i in range(size)])  140 us
    reduce_scatter x1, waiting for transfers between devices, local(): lax.psum_scatter(jnp.dot(left_full, filtered_full, preferred_element_type...  107 us
    all_gather x1, waiting for transfers between devices, local(): lax.all_gather(layer_rows(sparse, layers, level), 'row', axis=0, tiled=True)  90.5 us
    mul x6, local copies, waits for them, and re-layouts, local(): matrix.reshape(block_rows, BS, block_cols, BS)  38.7 us
    dot_general x1, matrix products, local(): jnp.dot(left_full, right_full, preferred_element_type=jnp.float32, precis...  31.1 us
    dot_general x1, matrix products, local(): jnp.dot(left_full, filtered_full, preferred_element_type=jnp.float32, pre...  29 us
    unnamed x16, local copies, waits for them, and re-layouts  19.1 us
  transfers between devices with their start and end apart: 7, of which 7 were waited for; matrix products, arithmetic and copies ran while one was open for 7% of the time, Pallas kernels for 0%

profile of v2, /device:TPU:0, one launch (start us, length us, event | category | flops | bytes accessed | tf_op | source)
XLA Modules:
  0.0 789.4 jit_solution(12203247749989544821)
XLA Ops:
  6.5 0.7 convert_element_type.6
  7.3 0.1 copy.5
  7.3 0.3 mul.66
  7.7 0.5 mul.67
  8.2 9.3 %copy.4 = f32[1024,2048]{0,1:T(8,128)} copy(f32[1024,2048]{1,0:T(8,128)} %param.3) | data formatting | bytes 16777216 | tf_op args[0]
  17.5 0.1 constant_dynamic-slice_fusion.3
  17.5 3.3 dynamic-slice_multiply_fusion.1
  20.8 0.0 all-gather.3.cloned.1.call-update
  20.8 0.0 all-gather.5.cloned.1.call-start
  20.9 0.3 mul.70
  21.2 0.5 mul.71
  21.7 0.1 constant_dynamic-slice_fusion.2
  21.8 3.2 dynamic-slice_multiply_fusion
  25.0 0.0 all-gather.5.cloned.1.call-update
  25.0 0.0 all-reduce.2.cloned.1.call-start
  25.1 12.3 %all-gather.3.cloned.1.call-done = f32[1024,1024]{0,1:T(8,128)} async-done(((f32[1024,512]{0,1:T(8,128)}), f32[1024,1024]{0,1:T(8,128)}) %all-gather.3.cloned.1.call-update) | async-done | bytes 4194320 | tf_op jit(solution)/shard_map/all_gather | solution.py:40
  37.4 90.5 %all-gather.5.cloned.1.call-done = f32[1024,2048]{1,0:T(8,128)} async-done(((f32[256,2048]{1,0:T(8,128)}), f32[1024,2048]{1,0:T(8,128)}) %all-gather.5.cloned.1.call-update) | async-done | bytes 8388624 | tf_op jit(solution)/shard_map/all_gather | solution.py:41
  127.9 31.1 %fusion.5 = f32[1024,2048]{1,0:T(8,128)} fusion(f32[1024,1024]{0,1:T(8,128)} %all-gather.3.cloned.1.call-done, f32[1024,2048]{1,0:T(8,128)} %all-gather.5.cloned.1.call-done), kind=kOutput, calls=%fused_computation.21 | convolution fusion | flops 25769803776 | bytes 20971520 | tf_op jit(solution)/shard_map/dot_general | solution.py:42
  159.0 0.0 all-reduce.2.cloned.1.call-update
  159.0 0.0 reduce-scatter.2.cloned.1.call-start
  159.1 0.6 copy-done.2
  159.7 4.4 mul.75
  164.1 8.0 %mul.76 = f32[256,2048]{1,0:T(8,128)} reshape(f32[8,32,64,32]{3,2,1,0:T(8,128)} %mul.75) | data formatting | bytes 4194304 | tf_op jit(solution)/shard_map/mul | solution.py:52
  172.0 278.0 %all-reduce.2.cloned.1.call-done = f32[8,4,32,2048]{3,2,1,0:T(8,128)} async-done(((f32[8,4,32,2048]{3,2,1,0:T(8,128)}), f32[8,4,32,2048]{3,2,1,0:T(8,128)}) %all-reduce.2.cloned.1.call-update) | async-done | bytes 8388624 | tf_op jit(solution)/shard_map/psum | solution.py:49
  450.0 1.7 constant_dynamic-slice_fusion.1
  451.7 1.8 bitcast_multiply_fusion
  453.5 1.5 collective-permute-start
  455.1 46.6 %collective-permute-done = f32[256,2048]{1,0:T(8,128)S(1)} collective-permute-done((f32[256,2048]{1,0:T(8,128)S(1)}, f32[256,2048]{1,0:T(8,128)S(1)}, u32[]{:S(2)}, u32[]{:S(2)}) %collective-permute-start) | collective-permute-done | bytes 2097184 | tf_op jit(solution)/shard_map/ppermute | solution.py:14
  501.7 1.3 copy-done
  503.0 0.6 collective-permute-start.1
  503.6 46.8 %collective-permute-done.1 = f32[256,2048]{1,0:T(8,128)} collective-permute-done((f32[256,2048]{1,0:T(8,128)S(1)}, f32[256,2048]{1,0:T(8,128)}, u32[]{:S(2)}, u32[]{:S(2)}) %collective-permute-start.1) | collective-permute-done | bytes 2097184 | tf_op jit(solution)/shard_map/ppermute | solution.py:14
  550.4 0.0 collective-permute-start.2
  550.4 46.7 %collective-permute-done.2 = f32[256,2048]{1,0:T(8,128)} collective-permute-done((f32[256,2048]{1,0:T(8,128)}, f32[256,2048]{1,0:T(8,128)}, u32[]{:S(2)}, u32[]{:S(2)}) %collective-permute-start.2) | collective-permute-done | bytes 2097184 | tf_op jit(solution)/shard_map/ppermute | solution.py:14
  597.1 1.8 constant_dynamic-update-slice_fusion.7
  598.9 1.8 constant_dynamic-update-slice_fusion.6
  600.7 0.1 constant_dynamic-update-slice_fusion.5
  600.9 0.1 constant_dynamic-update-slice_fusion.4
  601.0 2.0 constant_dynamic-update-slice_fusion.3
  603.0 1.8 constant_dynamic-update-slice_fusion.2
  604.8 0.1 constant_dynamic-update-slice_fusion.1
  605.0 0.1 constant_dynamic-update-slice_fusion
  605.1 0.0 copy-done.3
  605.1 29.0 %fusion = f32[1024,2048]{1,0:T(8,128)} fusion(f32[1024,1024]{0,1:T(8,128)S(1)} %copy-done.3, f32[2048,2048]{1,0:T(8,128)S(1)} %constant_dynamic-update-slice_fusion, s32[]{:T(128)S(6)} %select_n.28), kind=kOutput, calls=%fused_computation | convolution fusion | flops 25769803776 | bytes 20971524 | tf_op jit(solution)/shard_map/dot_general | solution.py:57
  634.1 0.0 reduce-scatter.2.cloned.1.call-update
  634.2 11.7 %mul.60 = f32[32,32,64,32]{3,2,1,0:T(8,128)} broadcast(f32[32,64]{1,0:T(8,128)S(1)} %convert_element_type.6), dimensions={0,2} | broadcast | bytes 8396800 | tf_op jit(solution)/shard_map/mul | solution.py:33
  645.8 25.4 %mul.61 = f32[1024,2048]{1,0:T(8,128)} reshape(f32[32,32,64,32]{3,2,1,0:T(8,128)} %mul.60) | data formatting | bytes 16777216 | tf_op jit(solution)/shard_map/mul | solution.py:33
  671.2 106.7 %reduce-scatter.2.cloned.1.call-done = f32[256,2048]{1,0:T(8,128)} async-done(((f32[1024,2048]{1,0:T(8,128)}), f32[256,2048]{1,0:T(8,128)}) %reduce-scatter.2.cloned.1.call-update) | async-done | bytes 2097168 | tf_op jit(solution)/shard_map/reduce_scatter | solution.py:56
  777.9 5.0 fusion.3
  (8 shorter events, 0.0 us)
Async XLA Ops:
  6.5 30.8 %all-gather.3.cloned.1.call-start = ((), (), s32[]{:S(2)}) async-start(), calls=%async_computation.1 | async-start | bytes 6291456 | tf_op jit(solution)/shard_map/all_gather | solution.py:40
  20.8 107.1 %all-gather.5.cloned.1.call-start = ((), (), s32[]{:S(2)}) async-start(), calls=%async_computation.2 | async-start | bytes 10485760 | tf_op jit(solution)/shard_map/all_gather | solution.py:41
  25.0 425.0 %all-reduce.2.cloned.1.call-start = ((), (), s32[]{:S(2)}) async-start(), calls=%async_computation.3 | async-start | bytes 16777216 | tf_op jit(solution)/shard_map/psum | solution.py:49
  159.0 0.7 copy-start.2
  159.0 618.9 %reduce-scatter.2.cloned.1.call-start = ((), (), s32[]{:S(2)}) async-start(), calls=%async_computation.4 | async-start | bytes 10485760 | tf_op jit(solution)/shard_map/reduce_scatter | solution.py:56
  453.5 48.2 %collective-permute-start = (f32[256,2048]{1,0:T(8,128)S(1)}, f32[256,2048]{1,0:T(8,128)S(1)}, u32[]{:S(2)}, u32[]{:S(2)}) collective-permute-start(f32[256,2048]{1,0:T(8,128)S(1)} %bitcast_multiply_fusion), channel_id=1, source_target_pairs={{0,8},{8,16},{16,24},{24,0},{1,9},{9,17},{17,25},{25,1},{2,10},{10... | collective-permute-start | bytes 6291464 | tf_op jit(solution)/shard_map/ppermute | solution.py:14
  501.7 1.3 copy-start
  503.0 47.4 %collective-permute-start.1 = (f32[256,2048]{1,0:T(8,128)S(1)}, f32[256,2048]{1,0:T(8,128)}, u32[]{:S(2)}, u32[]{:S(2)}) collective-permute-start(f32[256,2048]{1,0:T(8,128)S(1)} %collective-permute-done), channel_id=1, source_target_pairs={{0,8},{8,16},{16,24},{24,0},{1,9},{9,17},{17,25},{25,1},{2,10},{10... | collective-permute-start | bytes 6291464 | tf_op jit(solution)/shard_map/ppermute | solution.py:14
  550.4 46.7 %collective-permute-start.2 = (f32[256,2048]{1,0:T(8,128)}, f32[256,2048]{1,0:T(8,128)}, u32[]{:S(2)}, u32[]{:S(2)}) collective-permute-start(f32[256,2048]{1,0:T(8,128)} %collective-permute-done.1), channel_id=1, source_target_pairs={{0,8},{8,16},{16,24},{24,0},{1,9},{9,17},{17,25},{25,1},{2,10},{10... | collective-permute-start | bytes 6291464 | tf_op jit(solution)/shard_map/ppermute | solution.py:14
  550.4 50.3 %copy-start.1 = (f32[256,2048]{1,0:T(8,128)S(1)}, f32[256,2048]{1,0:T(8,128)}, u32[]{:S(2)}) copy-start(f32[256,2048]{1,0:T(8,128)} %copy-done) | copy-start | bytes 6291460
  601.0 4.1 copy-start.3
Sparse Core Ops, SparseCore 0:
  20.9 16.3 all-gather.2
  39.2 88.6 all-gather.4
  159.1 290.8 all-reduce.1
  634.3 143.5 reduce-scatter.1
